TPU v7x, 32 devices: a whole 2x2x4 slice. The times are simulated.
32 devices in a mesh: dp: 4 (over y, x), vocab: 8 (over z, core).
Axes of the slice: x: 2, y: 2, z: 4, core: 2. Of those that a mesh axis runs over, the one named last changes fastest.
Arguments:
- hidden: bfloat16 [256, 3072], P(('dp', 'vocab')), parts along dimension 0, may hold values from -60 to 60
- weight: bfloat16 [3072, 8192], P(None, 'vocab'), may hold values from -0.32421875 to 0.32421875
- targets: int32 [256], P('dp'), parts along dimension 0, may hold values from 0 to 8191
Outputs:
- loss: float32 [4], P('dp'), parts along dimension 0
- d_hidden: bfloat16 [256, 3072], P(('dp', 'vocab')), parts along dimension 0
- d_weight: bfloat16 [12288, 8192], P('dp', 'vocab'), parts along dimension 0
There are 4 independent parts, one for each index of `dp`. A program takes and returns all parts, laid end to end along the dimension named above; an argument that names none is the same for every part. Nothing has to cross between parts.
All inputs are finite; a program needn't handle non-finite values.
Results may differ from a plain program's by a relative error of at most 0.0035.
Values may be sent and summed in bfloat16 or wider, within the bound.
A program may use at most 64 MiB of HBM per device.

v0:
```python
import jax
import jax.numpy as jnp
from jax import lax
from jax.sharding import PartitionSpec as P


def joined(value, axis, combine):
    everything = jax.tree.map(lambda part: lax.all_gather(part, axis), value)
    initial = jax.tree.map(lambda part: part[0], everything)

    def hop(k, so_far):
        return combine(so_far, jax.tree.map(lambda part: part[k], everything))

    return lax.fori_loop(1, lax.axis_size(axis), hop, initial)


def combine_stats(first, second):
    top = jnp.maximum(first[0], second[0])
    total = first[1] * jnp.exp(first[0] - top) + second[1] * jnp.exp(second[0] - top)
    return (top, total, first[2] + second[2])


def body(hidden, weight, targets):
    gathered = lax.all_gather(hidden, "vocab", axis=0, tiled=True)
    logits = jnp.dot(gathered, weight, preferred_element_type=jnp.float32)
    width = weight.shape[1]
    offset = lax.axis_index("vocab") * width
    columns = offset + lax.broadcasted_iota(jnp.int32, (1, width), 1)
    hits = columns == targets[:, None]
    picked_local = jnp.sum(jnp.where(hits, logits, jnp.zeros_like(logits)), axis=1)
    local_top = jnp.max(logits, axis=1)
    local_total = jnp.sum(jnp.exp(logits - local_top[:, None]), axis=1)
    top, total, picked = joined((local_top, local_total, picked_local), "vocab", combine_stats)
    loss = jnp.mean(top + jnp.log(total) - picked).reshape(1)
    grad_logits = (
        jnp.exp(logits - top[:, None]) / total[:, None] - hits.astype(jnp.float32)
    ).astype(jnp.bfloat16)
    d_weight = lax.dot_general(
        gathered, grad_logits, (((0,), (0,)), ((), ())), preferred_element_type=jnp.float32
    ).astype(jnp.bfloat16)
    own_rows = hidden.shape[0]
    partial_value = lax.dot_general(
        grad_logits, weight, (((1,), (1,)), ((), ())), preferred_element_type=jnp.float32
    )
    everything = lax.psum(partial_value, "vocab")
    summed = lax.dynamic_slice_in_dim(everything, lax.axis_index("vocab") * own_rows, own_rows, 0)
    return (loss, summed.astype(jnp.bfloat16), d_weight)


def solution(mesh):
    placed = (P(("dp", "vocab"), None), P(None, "vocab"), P("dp"))
    return jax.shard_map(
        body,
        mesh=mesh,
        in_specs=placed,
        out_specs=(P("dp"), P(("dp", "vocab"), None), P("dp", "vocab")),
        check_vma=False,
    )
```

profile of v0, /device:TPU:0, one launch (start us, length us, event | category | flops | bytes accessed | tf_op | source)
XLA Modules:
  0.0 96.6 jit_solution(8625070616558614490)
XLA Ops:
  0.6 0.0 copy-start
  0.6 1.2 %dynamic-slice = u32[1]{0:T(128)} dynamic-slice(u32[32]{0:T(128)} %constant.59, u32[]{:T(128)S(6)} %add.78), dynamic_slice_sizes={1} | dynamic-slice | bytes 12
  2.6 16.4 %all_gather.21 = bf16[64,3072]{1,0:T(8,128)(2,1)S(1)} all-gather(bf16[8,3072]{1,0:T(8,128)(2,1)} %param.5), channel_id=1, replica_groups=mesh['dp'=4,'vocab'=8] {'vocab'}, dimensions={0}, use_global_device_ids=true | all-gather | bytes 442368 | tf_op jit(solution)/shard_map/all_gather | solution.py:24
  19.0 4.1 %fusion.14 = (f32[64]{0:T(128)S(1)}, f32[64,1024]{1,0:T(8,128)S(1)}) fusion(bf16[64,3072]{1,0:T(8,128)(2,1)S(1)} %all_gather.21, bf16[3072,1024]{1,0:T(8,128)(2,1)} %param.6), kind=kOutput, calls=%fused_computation.21 | convolution fusion | flops 402718656 | bytes 6947072 | tf_op jit(solution)/shard_map/dot_general | solution.py:25
  23.1 0.2 dynamic-update-slice
  23.4 0.0 copy-done
  23.4 0.2 fusion.7
  23.6 0.2 dynamic-update-slice.2
  23.8 0.2 dynamic-update-slice.1
  24.0 17.2 %all-reduce.3 = (f32[512]{0:T(512)S(1)}, f32[512]{0:T(512)S(1)}, f32[512]{0:T(512)S(1)}) all-reduce(f32[512]{0:T(512)S(1)} %dynamic-update-slice, f32[512]{0:T(512)S(1)} %dynamic-update-slice.1, f32[512]{0:T(512)S(1)} %dynamic-update-slice.2), channel_id=2, replica_groups=mesh['dp'=4,'vocab'=8] {'vocab'}, use_global_device_ids=true, to_apply=%add | all-reduce | flops 1536 | bytes 12288
  41.2 0.1 reshape.21
  41.3 0.1 reshape.20
  41.4 0.1 reshape.19
  41.5 0.3 while.19
  41.8 0.6 subtract_reduce_fusion
  43.0 4.8 %fusion.11 = f32[64,3072]{1,0:T(8,128)S(1)} fusion(bf16[3072,1024]{1,0:T(8,128)(2,1)} %param.6, f32[64,1024]{1,0:T(8,128)S(1)} %get-tuple-element.210, f32[64]{0:T(128)S(1)} %get-tuple-element.182, f32[64]{0:T(128)S(1)} %get-tuple-element.181, s32[1024]{0:T(1024)S(1)} %iota_add_fusion, s32[64]{0:T(128)S(1)} %copy-done), kind=kOutput, calls=%fused_computation.20 | convolution fusion | flops 403046400 | bytes 7344896 | tf_op jit(solution)/shard_map/dot_general | solution.py:42
  47.9 33.8 %all-reduce.5 = bf16[64,3072]{1,0:T(8,128)(2,1)S(1)} all-reduce(f32[64,3072]{1,0:T(8,128)S(1)} %fusion.11), channel_id=1, replica_groups=mesh['dp'=4,'vocab'=8] {'vocab'}, use_global_device_ids=true, to_apply=%region_6.7 | all-reduce | flops 196608 | bytes 1179648 | tf_op jit(solution)/shard_map/psum | solution.py:45
  81.7 0.6 dynamic-slice_convert_fusion
  82.3 4.6 %convert_bitcast_fusion = bf16[3072,1024]{0,1:T(8,128)(2,1)} fusion(bf16[64,3072]{1,0:T(8,128)(2,1)S(1)} %all_gather.21, f32[64,1024]{1,0:T(8,128)S(1)} %get-tuple-element.210, f32[64]{0:T(128)S(1)} %get-tuple-element.182, f32[64]{0:T(128)S(1)} %get-tuple-element.181, s32[1024]{0:T(1024)S(1)} %iota_add_fusion, s32[64]{0:T(128)S(1)} %copy-done), kind=kOutput, calls=%fused_computation.10 | convolution fusion | flops 406192128 | bytes 6951680 | tf_op jit(solution)/shard_map/dot_general | solution.py:38
  86.9 8.6 %copy.6 = bf16[3072,1024]{1,0:T(8,128)(2,1)} copy(bf16[3072,1024]{0,1:T(8,128)(2,1)} %convert_bitcast_fusion) | data formatting | bytes 12582912
  (14 shorter events, 0.2 us)
Async XLA Ops:
  0.6 22.7 %copy-start = (s32[64]{0:T(128)S(1)}, s32[64]{0:T(128)}, u32[]{:S(2)}) copy-start(s32[64]{0:T(128)} %param.7) | copy-start | bytes 772
where the time goes:
time: 97.1 us; the launch traced here: 96.6 us
  blocking collectives  67.4 us (69%)
  matrix products  13.5 us (14%)
  local copies, waits for them, and re-layouts  11.4 us (12%)
  between operations  3.16 us (3%)
  other arithmetic  1.03 us (1%)
    psum x1, blocking collectives, body(): everything = lax.psum(partial_value, 'vocab')  33.8 us
    unnamed x1, blocking collectives  17.2 us
    all_gather x1, blocking collectives, body(): gathered = lax.all_gather(hidden, 'vocab', axis=0, tiled=True)  16.4 us
    unnamed x10, local copies, waits for them, and re-layouts  10.6 us
    dot_general x1, matrix products, body(): lax.dot_general(grad_logits, weight, (((1,), (1,)), ((), ())), preferred_...  4.85 us
    dot_general x1, matrix products, body(): lax.dot_general(gathered, grad_logits, (((0,), (0,)), ((), ())), preferre...  4.58 us
    dot_general x1, matrix products, body(): logits = jnp.dot(gathered, weight, preferred_element_type=jnp.float32)  4.09 us

commit v1 on v0

--- a/solution.py
+++ b/solution.py
@@ -42,7 +42,7 @@
     partial_value = lax.dot_general(
         grad_logits, weight, (((1,), (1,)), ((), ())), preferred_element_type=jnp.float32
     )
-    everything = lax.psum(partial_value, "vocab")
+    everything = jnp.sum(lax.all_gather(partial_value, "vocab"), axis=0)
     summed = lax.dynamic_slice_in_dim(everything, lax.axis_index("vocab") * own_rows, own_rows, 0)
     return (loss, summed.astype(jnp.bfloat16), d_weight)
 

time: 97.1 us -> 129 us (1.33)
  waiting for transfers between devices: 0 us -> 48.8 us
  blocking collectives: 67.4 us -> 33.6 us
  between operations: 3.16 us -> 16.5 us
  other arithmetic: 1.03 us -> 4.25 us
    all_gather x0 -> x1, waiting for transfers between devices: none -> 48.7 us  [body(): everything = jnp.sum(lax.all_gather(partial_value, 'vocab'), axis=0)]
    psum x1 -> x0, blocking collectives: 33.8 us -> none  [body(): everything = lax.psum(partial_value, 'vocab')]
    reduce_sum x0 -> x1, other arithmetic: none -> 3.22 us  [body(): everything = jnp.sum(lax.all_gather(partial_value, 'vocab'), axis=0)]
  transfers between devices with their start and end apart: 0 -> 1, of which waited for: 0 -> 1; matrix products, arithmetic and copies ran while one was open for 0% -> 11% of each run, Pallas kernels for 0% -> 0%
where the time goes in v1:
time: 129 us
  waiting for transfers between devices  48.8 us (38%)
  blocking collectives  33.6 us (26%)
  between operations  16.5 us (13%)
  matrix products  14.5 us (11%)
  local copies, waits for them, and re-layouts  11.3 us (9%)
  other arithmetic  4.25 us (3%)
    all_gather x1, waiting for transfers between devices, body(): everything = jnp.sum(lax.all_gather(partial_value, 'vocab'), axis=0)  48.7 us
    unnamed x1, blocking collectives  17.2 us
    all_gather x1, blocking collectives, body(): gathered = lax.all_gather(hidden, 'vocab', axis=0, tiled=True)  16.4 us
    unnamed x10, local copies, waits for them, and re-layouts  10.4 us
    dot_general x1, matrix products, body(): lax.dot_general(grad_logits, weight, (((1,), (1,)), ((), ())), preferred_...  5.78 us
    dot_general x1, matrix products, body(): lax.dot_general(gathered, grad_logits, (((0,), (0,)), ((), ())), preferre...  4.58 us
    dot_general x1, matrix products, body(): logits = jnp.dot(gathered, weight, preferred_element_type=jnp.float32)  4.09 us
    reduce_sum x1, other arithmetic, body(): everything = jnp.sum(lax.all_gather(partial_value, 'vocab'), axis=0)  3.22 us
  transfers between devices with their start and end apart: 1, of which 1 were waited for; matrix products, arithmetic and copies ran while one was open for 11% of the time, Pallas kernels for 0%

profile of v1, /device:TPU:0, one launch (start us, length us, event | category | flops | bytes accessed | tf_op | source)
XLA Modules:
  0.0 129.0 jit_solution(5680609029893360331)
XLA Ops:
  7.2 0.0 copy-start
  7.2 0.0 all-gather.6.cloned.1.call-start
  7.2 16.4 %all_gather.27 = bf16[64,3072]{1,0:T(8,128)(2,1)S(1)} all-gather(bf16[8,3072]{1,0:T(8,128)(2,1)} %param.5), channel_id=1, replica_groups=mesh['dp'=4,'vocab'=8] {'vocab'}, dimensions={0}, use_global_device_ids=true | all-gather | bytes 442368 | tf_op jit(solution)/shard_map/all_gather | solution.py:24
  23.7 1.2 dynamic-slice
  25.6 4.1 %fusion.14 = (f32[64]{0:T(128)S(1)}, f32[64,1024]{1,0:T(8,128)S(1)}) fusion(bf16[64,3072]{1,0:T(8,128)(2,1)S(1)} %all_gather.27, bf16[3072,1024]{1,0:T(8,128)(2,1)} %param.6), kind=kOutput, calls=%fused_computation.21 | convolution fusion | flops 402718656 | bytes 6947072 | tf_op jit(solution)/shard_map/dot_general | solution.py:25
  29.7 0.2 dynamic-update-slice
  29.9 0.0 copy-done
  29.9 0.2 fusion.7
  30.2 0.2 dynamic-update-slice.2
  30.4 0.2 dynamic-update-slice.1
  30.6 17.2 %all-reduce.3 = (f32[512]{0:T(512)S(1)}, f32[512]{0:T(512)S(1)}, f32[512]{0:T(512)S(1)}) all-reduce(f32[512]{0:T(512)S(1)} %dynamic-update-slice, f32[512]{0:T(512)S(1)} %dynamic-update-slice.1, f32[512]{0:T(512)S(1)} %dynamic-update-slice.2), channel_id=2, replica_groups=mesh['dp'=4,'vocab'=8] {'vocab'}, use_global_device_ids=true, to_apply=%add | all-reduce | flops 1536 | bytes 12288
  47.8 0.1 reshape.21
  47.9 0.1 reshape.20
  47.9 0.1 reshape.19
  48.0 0.3 while.19
  48.3 5.8 %fusion.11 = f32[64,3072]{1,0:T(8,128)} fusion(bf16[3072,1024]{1,0:T(8,128)(2,1)} %param.6, f32[64,1024]{1,0:T(8,128)S(1)} %get-tuple-element.210, f32[64]{0:T(128)S(1)} %get-tuple-element.182, f32[64]{0:T(128)S(1)} %get-tuple-element.181, s32[1024]{0:T(1024)S(1)} %iota_add_fusion, s32[64]{0:T(128)S(1)} %copy-done), kind=kOutput, calls=%fused_computation.20 | convolution fusion | flops 403046400 | bytes 7344896 | tf_op jit(solution)/shard_map/dot_general | solution.py:42
  54.1 0.0 all-gather.6.cloned.1.call-update
  54.1 4.6 %convert_bitcast_fusion = bf16[3072,1024]{0,1:T(8,128)(2,1)} fusion(bf16[64,3072]{1,0:T(8,128)(2,1)S(1)} %all_gather.27, f32[64,1024]{1,0:T(8,128)S(1)} %get-tuple-element.210, f32[64]{0:T(128)S(1)} %get-tuple-element.182, f32[64]{0:T(128)S(1)} %get-tuple-element.181, s32[1024]{0:T(1024)S(1)} %iota_add_fusion, s32[64]{0:T(128)S(1)} %copy-done), kind=kOutput, calls=%fused_computation.10 | convolution fusion | flops 406192128 | bytes 6951680 | tf_op jit(solution)/shard_map/dot_general | solution.py:38
  58.7 8.5 %copy.6 = bf16[3072,1024]{1,0:T(8,128)(2,1)} copy(bf16[3072,1024]{0,1:T(8,128)(2,1)} %convert_bitcast_fusion) | data formatting | bytes 12582912
  67.2 0.6 subtract_reduce_fusion
  68.4 48.7 %all-gather.6.cloned.1.call-done = f32[512,3072]{1,0:T(8,128)} async-done(((f32[64,3072]{1,0:T(8,128)}), f32[512,3072]{1,0:T(8,128)}) %all-gather.6.cloned.1.call-update) | async-done | bytes 6291472 | tf_op jit(solution)/shard_map/all_gather | solution.py:45
  117.2 3.2 %reduce_sum.39 = bf16[64,3072]{1,0:T(8,128)(2,1)S(1)} reduce(f32[8,64,3072]{2,1,0:T(8,128)} %bitcast.28, f32[]{:T(128)} %constant.50.clone.1), dimensions={0}, to_apply=%region_6.7 | reduce | flops 1376256 | bytes 6684676 | tf_op jit(solution)/shard_map/reduce_sum | solution.py:45
  120.4 0.6 dynamic-slice_convert_fusion
  (14 shorter events, 0.2 us)
Async XLA Ops:
  7.2 22.8 %copy-start = (s32[64]{0:T(128)S(1)}, s32[64]{0:T(128)}, u32[]{:S(2)}) copy-start(s32[64]{0:T(128)} %param.7) | copy-start | bytes 772
  7.2 110.0 %all-gather.6.cloned.1.call-start = ((), (), s32[]{:S(2)}) async-start(), calls=%async_computation | async-start | bytes 7077888 | tf_op jit(solution)/shard_map/all_gather | solution.py:45
Sparse Core Ops, SparseCore 0:
  54.2 62.8 all-gather.5
